TPU v7x, 32 devices: a whole 2x2x4 slice. The times are simulated.
32 devices in a mesh: gx: 4 (over y, core), gy: 4 (over z), gz: 2 (over x).
Axes of the slice: x: 2, y: 2, z: 4, core: 2. Of those that a mesh axis runs over, the one named last changes fastest.
Arguments:
- fractions: float32 [3, 4, 8, 4, 128], P(None, 'gx', 'gy', 'gz'), may hold values from 0 to 1
- polarizability: float32 [4, 8, 4, 128], P('gx', 'gy', 'gz'), may hold values from 0.5 to 2
- occupancy: int32 [4, 8, 4, 128], P('gx', 'gy', 'gz'), may hold values 0 or 1
- pair_mask: int32 [4, 8, 4, 27], P('gx', 'gy', 'gz'), may hold values from 0 to 1, as said below
- perm_field: float32 [6, 4, 8, 4, 128], P(None, 'gx', 'gy', 'gz'), may hold values from -6 to 6
- history: float32 [6, 6, 4, 8, 4, 128], P(None, None, 'gx', 'gy', 'gz'), may hold values from -12 to 12
Outputs:
- induced: float32 [6, 4, 8, 4, 128], P(None, 'gx', 'gy', 'gz')
- change: float32 [], replicated
Inputs may be any that keep to these rules, and one draw needn't show every extreme that they name: pair_mask[t, k] equals pair_mask at tile t + offset(k) for the opposite offset 26 - k (periodic); pair_mask[t, 13] (the tile itself) is 1.
All inputs are finite; a program needn't handle non-finite values. No bound on the sum of `occupancy` on one device may be relied on, other than what follows from the above.
Results may differ from a plain program's by a relative error of at most 0.0003.
Values sent between devices are 32-bit elements; how exact they have to be, the bound alone decides.
A program may use at most 64 MiB of HBM per device.

v0:
```python
import jax
import jax.numpy as jnp
from jax import lax
from jax.sharding import PartitionSpec as P

CELL_EDGE = 10.0
SOFTENING = 0.3
THOLE_DAMP = 0.39
RELAXATION = 0.7


def with_halo(cells, sides, width):
    for axis, dim in sides:
        count = lax.axis_size(axis)
        head = lax.slice_in_dim(cells, 0, width, axis=dim)
        tail = lax.slice_in_dim(cells, cells.shape[dim] - width, cells.shape[dim], axis=dim)
        cells = jnp.concatenate(
            [
                lax.ppermute(tail, axis, [(i, (i + 1) % count) for i in range(count)]),
                cells,
                lax.ppermute(head, axis, [((i + 1) % count, i) for i in range(count)]),
            ],
            axis=dim,
        )
    return cells


def pair_field(target, source, moment, offset_vec, itself, allowed):
    displace = [
        (offset_vec[axis_num] + source[axis_num][:, None, :] - target[axis_num][:, :, None])
        * CELL_EDGE
        for axis_num in range(3)
    ]
    dist_sq = (
        displace[0] * displace[0]
        + displace[1] * displace[1]
        + displace[2] * displace[2]
        + SOFTENING
    )
    inv_cube = lax.rsqrt(dist_sq) / dist_sq
    thole_arg = (
        dist_sq * jnp.sqrt(dist_sq) * lax.rsqrt(target[3][:, :, None] * source[3][:, None, :])
    )
    damping = jnp.exp(-THOLE_DAMP * thole_arg)
    lambda_three = 1.0 - damping
    lambda_five = 1.0 - (1.0 + THOLE_DAMP * thole_arg) * damping
    slots = target.shape[-1]
    self_pair = jnp.logical_and(itself, jnp.eye(slots, dtype=bool))
    weight = jnp.where(self_pair, 0.0, allowed[:, None, None])
    radial = 3.0 * lambda_five * inv_cube / dist_sq * weight
    direct = lambda_three * inv_cube * weight
    fields = []
    for which_set in range(moment.shape[0] // 3):
        parts = [moment[3 * which_set + axis_num][:, None, :] for axis_num in range(3)]
        project = displace[0] * parts[0] + displace[1] * parts[1] + displace[2] * parts[2]
        for axis_num in range(3):
            fields.append(
                jnp.sum(radial * project * displace[axis_num] - direct * parts[axis_num], axis=-1)
            )
    return jnp.stack(fields)


def slab_field(geometry_pad, moment_pad, allowed_slab, slab_index):
    width_y = geometry_pad.shape[2] - 2
    width_z = geometry_pad.shape[3] - 2
    slots = geometry_pad.shape[4]
    rows = moment_pad.shape[0]
    zero = jnp.zeros((), jnp.int32)
    one = jnp.ones((), jnp.int32)
    first_x = (jnp.asarray(slab_index) + 1).astype(jnp.int32)
    target = lax.dynamic_slice(
        geometry_pad, (zero, first_x, one, one, zero), (4, 1, width_y, width_z, slots)
    ).reshape(4, width_y * width_z, slots)

    def offset_step(offset, summed):
        offset = jnp.asarray(offset).astype(jnp.int32)
        along_x = offset // 9 - 1
        along_y = offset // 3 % 3 - 1
        along_z = offset % 3 - 1
        starts = (zero, first_x + along_x, one + along_y, one + along_z, zero)
        source = lax.dynamic_slice(geometry_pad, starts, (4, 1, width_y, width_z, slots)).reshape(
            4, width_y * width_z, slots
        )
        moment = lax.dynamic_slice(moment_pad, starts, (rows, 1, width_y, width_z, slots)).reshape(
            rows, width_y * width_z, slots
        )
        allowed = (
            lax.dynamic_index_in_dim(allowed_slab, offset, 2, keepdims=False)
            .reshape(-1)
            .astype(jnp.float32)
        )
        offset_vec = jnp.stack([along_x, along_y, along_z]).astype(jnp.float32)
        return summed + pair_field(target, source, moment, offset_vec, offset == 13, allowed)

    summed = lax.fori_loop(
        0, 27, offset_step, jnp.zeros((rows, width_y * width_z, slots), jnp.float32)
    )
    return summed.reshape(rows, width_y, width_z, slots)


def device_field(geometry_pad, moment_pad, pair_mask):
    slabs = [slab_field(geometry_pad, moment_pad, pair_mask[0], 0)]
    return jnp.stack(slabs, 1)


def share_dipoles(dipoles):
    return with_halo(dipoles, (("gx", 1), ("gy", 2), ("gz", 3)), 1)


def global_gram(local_gram):
    return lax.psum(local_gram, ("gx", "gy", "gz"))


def fit_coefficients(gram_matrix):
    past_count = gram_matrix.shape[0] - 1
    gram_past = gram_matrix[:past_count, :past_count]
    gram_next = gram_matrix[:past_count, past_count]
    ridge_term = 0.001 * jnp.trace(gram_past) / past_count + 1.0
    factor = jnp.linalg.cholesky(gram_past + ridge_term * jnp.eye(past_count, dtype=jnp.float32))
    return jax.scipy.linalg.cho_solve((factor, True), gram_next)


def on_device(fractions, polarizability, occupancy, pair_mask, perm_field, history):
    filled = occupancy.astype(jnp.float32)
    geometry = jnp.concatenate([fractions, polarizability[None]], 0)
    masked = history * filled
    past_sets = masked.shape[0]
    flat_hist = masked.reshape(past_sets, -1)
    local_gram = jnp.dot(flat_hist, flat_hist.T, precision=lax.Precision.HIGHEST)
    scaled = RELAXATION * filled * polarizability
    later = masked[1:]
    coeffs = fit_coefficients(global_gram(local_gram))
    geometry_pad = with_halo(geometry, (("gx", 1), ("gy", 2), ("gz", 3)), 1)
    predicted = jnp.tensordot(coeffs, later, axes=1, precision=lax.Precision.HIGHEST)
    field_one = device_field(geometry_pad, share_dipoles(predicted), pair_mask)
    dipole_one = (1.0 - RELAXATION) * predicted + scaled * (perm_field + field_one)
    field_two = device_field(geometry_pad, share_dipoles(dipole_one), pair_mask)
    induced = (1.0 - RELAXATION) * dipole_one + scaled * (perm_field + field_two)
    update = induced - dipole_one
    totals = lax.psum((jnp.sum(update * update), jnp.sum(induced * induced)), ("gx", "gy", "gz"))
    change = jnp.sqrt(totals[0] / (totals[1] + 1.0))
    return (induced, change)


def solution(mesh):
    in_specs = (
        P(None, "gx", "gy", "gz", None),
        P("gx", "gy", "gz", None),
        P("gx", "gy", "gz", None),
        P("gx", "gy", "gz", None),
        P(None, "gx", "gy", "gz", None),
        P(None, None, "gx", "gy", "gz", None),
    )
    out_specs = (P(None, "gx", "gy", "gz", None), P())
    return jax.shard_map(
        on_device, mesh=mesh, in_specs=in_specs, out_specs=out_specs, check_vma=False
    )
```

profile of v0, /device:TPU:12, one launch (start us, length us, event | category | flops | bytes accessed | tf_op | source)
XLA Modules:
  0.0 395.9 jit_solution(7175893039068339655)
XLA Ops:
  3.1 41.2 %psum.21 = f32[6,6]{0,1:T(8,128)S(1)} all-reduce(f32[6,6]{0,1:T(8,128)S(1)} %convolution_bitcast_fusion), channel_id=1, replica_groups=mesh['gx'=4,'gy'=4,'gz'=2] {'gx','gy','gz'}, use_global_device_ids=true, to_apply=%region_0.0 | all-reduce | flops 36 | bytes 288 | tf_op jit(solution)/shard_map/psum | solution.py:111
  66.1 134.4 %while.38 = (s32[]{:T(128)}, f32[6,4,128]{2,1,0:T(4,128)S(1)}, f32[4,3,4,4,128]{4,3,2,1,0:T(4,128)S(1)}, f32[4,4,128]{2,1,0:T(4,128)S(1)}, s32[2,2,27]{1,0,2:T(2...) while((s32[]{:T(128)}, f32[6,4,128]{2,1,0:T(4,128)S(1)}, ...), condition=%wide.region_11.12_spmd.clone, body=%wide.region_4.11_spmd.clone.sunk | while | flops 6200888 | bytes 287493 | solution.py:95
  203.8 2.3 collective-permute-start.14
  208.6 2.6 collective-permute-done.15
  213.4 2.1 collective-permute-done.16
  216.8 133.6 %while.39 = (s32[]{:T(128)}, f32[6,4,128]{2,1,0:T(4,128)S(1)}, f32[4,3,4,4,128]{4,3,2,1,0:T(4,128)S(1)}, f32[4,4,128]{2,1,0:T(4,128)S(1)}, s32[2,2,27]{1,0,2:T(2...) while((s32[]{:T(128)}, f32[6,4,128]{2,1,0:T(4,128)S(1)}, ...), condition=%wide.region_19.20_spmd.clone, body=%wide.region_12.19_spmd.clone.sunk | while | flops 6200890 | bytes 262953 | solution.py:95
  217.7 1.9 constant_dynamic-slice_fusion.14
  222.6 1.9 constant_dynamic-slice_fusion.14
  227.5 1.9 constant_dynamic-slice_fusion.14
  232.5 1.9 constant_dynamic-slice_fusion.14
  237.4 1.9 constant_dynamic-slice_fusion.14
  242.4 1.9 constant_dynamic-slice_fusion.14
  247.3 1.9 constant_dynamic-slice_fusion.14
  252.3 1.9 constant_dynamic-slice_fusion.14
  257.2 1.9 constant_dynamic-slice_fusion.14
  262.2 1.9 constant_dynamic-slice_fusion.14
  267.1 1.9 constant_dynamic-slice_fusion.14
  272.1 1.9 constant_dynamic-slice_fusion.14
  277.0 1.9 constant_dynamic-slice_fusion.14
  282.0 1.9 constant_dynamic-slice_fusion.14
  286.9 1.9 constant_dynamic-slice_fusion.14
  291.9 1.9 constant_dynamic-slice_fusion.14
  296.8 1.9 constant_dynamic-slice_fusion.14
  301.8 1.9 constant_dynamic-slice_fusion.14
  306.7 1.9 constant_dynamic-slice_fusion.14
  311.7 1.9 constant_dynamic-slice_fusion.14
  316.6 1.9 constant_dynamic-slice_fusion.14
  321.6 1.9 constant_dynamic-slice_fusion.14
  326.5 1.9 constant_dynamic-slice_fusion.14
  331.5 1.9 constant_dynamic-slice_fusion.14
  336.4 1.9 constant_dynamic-slice_fusion.14
  351.8 41.8 %all-reduce = (f32[]{:T(128)}, f32[]{:T(128)}) all-reduce(f32[]{:T(128)} %get-tuple-element.589, f32[]{:T(128)} %get-tuple-element.588), channel_id=1, replica_groups=mesh['gx'=4,'gy'=4,'gz'=2] {'gx','gy','gz'}, use_global_device_ids=true, to_apply=%region_21.22 | all-reduce | flops 2 | bytes 16 | tf_op jit(solution)/shard_map/psum | solution.py:140
  (1250 shorter events, 242.9 us)
Async XLA Ops:
  2.2 0.9 copy-start
  48.5 2.1 copy-start.1
  48.7 1.8 copy-start.2
  48.7 7.1 %collective-permute-start.6 = (f32[6,1,2,2,128]{4,3,2,0,1:T(2,128)S(1)}, f32[6,1,2,2,128]{4,3,2,0,1:T(2,128)S(1)}, u32[]{:S(2)}, u32[]{:S(2)}) collective-permute-start(f32[6,1,2,2,128]{4,3,2,0,1:T(2,128)S(1)} %bitcast.219), channel_id=1, source_target_pairs={{0,8},{8,16},{16,24},{24,0},{1,9},{9,17},{17,25},{25,1},{2,10},{10... | collective-permute-start | bytes 36872 | tf_op jit(solution)/shard_map/ppermute | solution.py:19
  48.8 7.0 %collective-permute-start.7 = (f32[6,1,2,2,128]{4,3,2,0,1:T(2,128)S(1)}, f32[6,1,2,2,128]{4,3,2,0,1:T(2,128)S(1)}, u32[]{:S(2)}, u32[]{:S(2)}) collective-permute-start(f32[6,1,2,2,128]{4,3,2,0,1:T(2,128)S(1)} %bitcast.220), channel_id=1, source_target_pairs={{8,0},{16,8},{24,16},{0,24},{9,1},{17,9},{25,17},{1,25},{10,2},{18... | collective-permute-start | bytes 36872 | tf_op jit(solution)/shard_map/ppermute | solution.py:21
  50.5 1.8 copy-start.4
  50.6 3.2 collective-permute-start
  50.6 3.1 collective-permute-start.1
  52.4 0.7 copy-start.5
  53.8 4.6 %collective-permute-start.2 = (f32[4,3,1,2,128]{4,3,2,1,0:T(2,128)S(1)}, f32[4,3,1,2,128]{4,3,2,1,0:T(2,128)S(1)}, u32[]{:S(2)}, u32[]{:S(2)}) collective-permute-start(f32[4,3,1,2,128]{4,3,2,1,0:T(2,128)S(1)} %get-tuple-element.669), channel_id=1, source_target_pairs={{0,2},{2,4},{4,6},{6,0},{1,3},{3,5},{5,7},{7,1},{8,10},{10,12},{12... | collective-permute-start | bytes 36872 | tf_op jit(solution)/shard_map/ppermute | solution.py:19
  55.2 3.7 collective-permute-start.3
  55.9 5.2 %collective-permute-start.8 = (f32[6,3,1,2,128]{4,3,2,0,1:T(2,128)S(1)}, f32[6,3,1,2,128]{4,3,2,0,1:T(2,128)S(1)}, u32[]{:S(2)}, u32[]{:S(2)}) collective-permute-start(f32[6,3,1,2,128]{4,3,2,0,1:T(2,128)S(1)} %get-tuple-element.667), channel_id=1, source_target_pairs={{0,2},{2,4},{4,6},{6,0},{1,3},{3,5},{5,7},{7,1},{8,10},{10,12},{12... | collective-permute-start | bytes 55304 | tf_op jit(solution)/shard_map/ppermute | solution.py:19
  57.3 3.8 collective-permute-start.9
  59.0 4.4 %collective-permute-start.4 = (f32[4,3,4,1,128]{4,3,2,1,0:T(1,128)S(1)}, f32[4,3,4,1,128]{4,3,2,1,0:T(1,128)S(1)}, u32[]{:S(2)}, u32[]{:S(2)}) collective-permute-start(f32[4,3,4,1,128]{4,3,2,1,0:T(1,128)S(1)} %get-tuple-element.663), channel_id=1, source_target_pairs={{0,1},{1,0},{2,3},{3,2},{4,5},{5,4},{6,7},{7,6},{8,9},{9,8},{10,11... | collective-permute-start | bytes 73736 | tf_op jit(solution)/shard_map/ppermute | solution.py:19
  59.8 3.8 collective-permute-start.5
  61.2 4.0 %collective-permute-start.10 = (f32[6,3,4,1,128]{4,3,2,0,1:T(1,128)S(1)}, f32[6,3,4,1,128]{4,3,2,0,1:T(1,128)S(1)}, u32[]{:S(2)}, u32[]{:S(2)}) collective-permute-start(f32[6,3,4,1,128]{4,3,2,0,1:T(1,128)S(1)} %get-tuple-element.661), channel_id=1, source_target_pairs={{0,1},{1,0},{2,3},{3,2},{4,5},{5,4},{6,7},{7,6},{8,9},{9,8},{10,11... | collective-permute-start | bytes 110600 | tf_op jit(solution)/shard_map/ppermute | solution.py:19
  62.0 4.0 collective-permute-start.11
  66.1 134.4 %copy-start.3 = (f32[6,1,2,2,128]{4,3,2,1,0:T(2,128)S(1)}, f32[6,1,2,2,128]{4,3,2,1,0:T(2,128)}, u32[]{:S(2)}) copy-start(f32[6,1,2,2,128]{4,3,2,1,0:T(2,128)} %param.14) | copy-start | bytes 36868
  200.5 3.2 collective-permute-start.12
  200.6 3.1 collective-permute-start.13
  203.8 4.9 %collective-permute-start.14 = (f32[6,3,1,2,128]{4,3,2,1,0:T(2,128)S(1)}, f32[6,3,1,2,128]{4,3,2,1,0:T(2,128)S(1)}, u32[]{:S(2)}, u32[]{:S(2)}) collective-permute-start(f32[6,3,1,2,128]{4,3,2,1,0:T(2,128)S(1)} %get-tuple-element.665), channel_id=1, source_target_pairs={{0,2},{2,4},{4,6},{6,0},{1,3},{3,5},{5,7},{7,1},{8,10},{10,12},{12... | collective-permute-start | bytes 55304 | tf_op jit(solution)/shard_map/ppermute | solution.py:19
  206.1 5.1 %collective-permute-start.15 = (f32[6,3,1,2,128]{4,3,2,1,0:T(2,128)S(1)}, f32[6,3,1,2,128]{4,3,2,1,0:T(2,128)S(1)}, u32[]{:S(2)}, u32[]{:S(2)}) collective-permute-start(f32[6,3,1,2,128]{4,3,2,1,0:T(2,128)S(1)} %get-tuple-element.666), channel_id=1, source_target_pairs={{2,0},{4,2},{6,4},{0,6},{3,1},{5,3},{7,5},{1,7},{10,8},{12,10},{14... | collective-permute-start | bytes 55304 | tf_op jit(solution)/shard_map/ppermute | solution.py:21
  211.3 4.2 %collective-permute-start.16 = (f32[6,3,4,1,128]{4,3,2,1,0:T(1,128)S(1)}, f32[6,3,4,1,128]{4,3,2,1,0:T(1,128)S(1)}, u32[]{:S(2)}, u32[]{:S(2)}) collective-permute-start(f32[6,3,4,1,128]{4,3,2,1,0:T(1,128)S(1)} %get-tuple-element.659), channel_id=1, source_target_pairs={{0,1},{1,0},{2,3},{3,2},{4,5},{5,4},{6,7},{7,6},{8,9},{9,8},{10,11... | collective-permute-start | bytes 110600 | tf_op jit(solution)/shard_map/ppermute | solution.py:19
  212.8 4.0 collective-permute-start.17
where the time goes:
time: 398 us; the launch traced here: 396 us
  other arithmetic  220 us (55%)
  blocking collectives  83 us (21%)
  local copies, waits for them, and re-layouts  45.7 us (11%)
  starting transfers between devices  19.3 us (5%)
  waiting for transfers between devices  12.7 us (3%)
  loops' own time  10.9 us (3%)
    reduce_sum x108, other arithmetic, pair_field(): jnp.sum(radial * project * displace[axis_num] - direct * parts[axis_num],...  102 us
    slice x27, other arithmetic, pair_field(): moment[3 * which_set + axis_num][:, None, :]  52 us
    add x27, other arithmetic, pair_field(): offset_vec[axis_num] + source[axis_num][:, None, :]  51.6 us
    psum x1, blocking collectives, on_device(): lax.psum((jnp.sum(update * update), jnp.sum(induced * induced)), ('gx', '...  41.8 us
    psum x1, blocking collectives, global_gram(): return lax.psum(local_gram, ('gx', 'gy', 'gz'))  41.2 us
    slice x54, local copies, waits for them, and re-layouts, pair_field(): offset_vec[axis_num] + source[axis_num][:, None, :]  36 us
    ppermute x9, starting transfers between devices, with_halo(): lax.ppermute(head, axis, [((i + 1) % count, i) for i in range(count)])  10.9 us
    another operation x2, loops' own time, slab_field(): lax.fori_loop(0, 27, offset_step, jnp.zeros((rows, width_y * width_z, slo...  10.9 us
  transfers between devices with their start and end apart: 18, of which 11 were waited for; matrix products, arithmetic and copies ran while one was open for 0% of the time, Pallas kernels for 0%

commit v1 on v0

--- a/solution.py
+++ b/solution.py
@@ -7,6 +7,12 @@
 SOFTENING = 0.3
 THOLE_DAMP = 0.39
 RELAXATION = 0.7
+
+
+def gather_and_add(x, axis):
+    parts = lax.all_gather(x, axis, axis=0, tiled=False)
+    total = parts.sum(axis=0)
+    return total
 
 
 def with_halo(cells, sides, width):
@@ -108,7 +114,7 @@
 
 
 def global_gram(local_gram):
-    return lax.psum(local_gram, ("gx", "gy", "gz"))
+    return gather_and_add(local_gram, ("gx", "gy", "gz"))
 
 
 def fit_coefficients(gram_matrix):

time: 398 us -> 425 us (1.068)
  blocking collectives: 83 us -> 108 us
    all_gather x0 -> x1, blocking collectives: none -> 65.1 us  [gather_and_add(): parts = lax.all_gather(x, axis, axis=0, tiled=False)]
    psum x1 -> x0, blocking collectives: 41.2 us -> none  [global_gram(): return lax.psum(local_gram, ('gx', 'gy', 'gz'))]
    ppermute x9, starting transfers between devices: 10.9 us -> 17.6 us  [with_halo(): lax.ppermute(head, axis, [((i + 1) % count, i) for i in range(count)])]
  transfers between devices with their start and end apart: 18 -> 18, of which waited for: 11 -> 9; matrix products, arithmetic and copies ran while one was open for 0% -> 0% of each run, Pallas kernels for 0% -> 0%
where the time goes in v1:
time: 425 us; the launch traced here: 423 us
  other arithmetic  220 us (52%)
  blocking collectives  108 us (25%)
  local copies, waits for them, and re-layouts  45.4 us (11%)
  starting transfers between devices  22.8 us (5%)
  waiting for transfers between devices  12.1 us (3%)
  loops' own time  10.9 us (3%)
    reduce_sum x108, other arithmetic, pair_field(): jnp.sum(radial * project * displace[axis_num] - direct * parts[axis_num],...  102 us
    all_gather x1, blocking collectives, gather_and_add(): parts = lax.all_gather(x, axis, axis=0, tiled=False)  65.1 us
    slice x27, other arithmetic, pair_field(): moment[3 * which_set + axis_num][:, None, :]  52 us
    add x27, other arithmetic, pair_field(): offset_vec[axis_num] + source[axis_num][:, None, :]  51.6 us
    psum x1, blocking collectives, on_device(): lax.psum((jnp.sum(update * update), jnp.sum(induced * induced)), ('gx', '...  42.7 us
    slice x54, local copies, waits for them, and re-layouts, pair_field(): offset_vec[axis_num] + source[axis_num][:, None, :]  36 us
    ppermute x9, starting transfers between devices, with_halo(): lax.ppermute(head, axis, [((i + 1) % count, i) for i in range(count)])  17.6 us
    another operation x2, loops' own time, slab_field(): lax.fori_loop(0, 27, offset_step, jnp.zeros((rows, width_y * width_z, slo...  10.9 us
  transfers between devices with their start and end apart: 18, of which 9 were waited for; matrix products, arithmetic and copies ran while one was open for 0% of the time, Pallas kernels for 0%

profile of v1, /device:TPU:12, one launch (start us, length us, event | category | flops | bytes accessed | tf_op | source)
XLA Modules:
  0.0 423.3 jit_solution(191777927832230305)
XLA Ops:
  2.6 65.1 %all-gather.1 = f32[32,6,6]{2,1,0:T(8,128)S(1)} all-gather(f32[1,6,6]{2,1,0:T(8,128)S(1)} %convolution_bitcast_fusion), channel_id=2, replica_groups=mesh['gx'=4,'gy'=4,'gz'=2] {'gx','gy','gz'}, dimensions={0}, use_global_device_ids=true | all-gather | bytes 4752 | tf_op jit(solution)/shard_map/all_gather | solution.py:13
  77.5 3.3 collective-permute-start.3
  81.0 3.8 collective-permute-start.9
  85.0 2.0 collective-permute-start.5
  87.2 1.9 collective-permute-start.11
  91.6 134.4 %while.38 = (s32[]{:T(128)}, f32[6,4,128]{2,1,0:T(4,128)S(1)}, f32[4,3,4,4,128]{4,3,2,1,0:T(4,128)S(1)}, f32[4,4,128]{2,1,0:T(4,128)S(1)}, s32[2,2,27]{1,0,2:T(2...) while((s32[]{:T(128)}, f32[6,4,128]{2,1,0:T(4,128)S(1)}, ...), condition=%wide.region_11.12_spmd.clone, body=%wide.region_4.11_spmd.clone.sunk | while | flops 6200888 | bytes 287493 | solution.py:101
  229.3 3.0 collective-permute-start.14
  234.9 2.6 collective-permute-done.15
  239.6 1.9 collective-permute-done.16
  243.3 133.6 %while.39 = (s32[]{:T(128)}, f32[6,4,128]{2,1,0:T(4,128)S(1)}, f32[4,3,4,4,128]{4,3,2,1,0:T(4,128)S(1)}, f32[4,4,128]{2,1,0:T(4,128)S(1)}, s32[2,2,27]{1,0,2:T(2...) while((s32[]{:T(128)}, f32[6,4,128]{2,1,0:T(4,128)S(1)}, ...), condition=%wide.region_19.20_spmd.clone, body=%wide.region_12.19_spmd.clone.sunk | while | flops 6200890 | bytes 262953 | solution.py:101
  244.1 1.9 constant_dynamic-slice_fusion.14
  249.1 1.9 constant_dynamic-slice_fusion.14
  254.0 1.9 constant_dynamic-slice_fusion.14
  259.0 1.9 constant_dynamic-slice_fusion.14
  263.9 1.9 constant_dynamic-slice_fusion.14
  268.8 1.9 constant_dynamic-slice_fusion.14
  273.8 1.9 constant_dynamic-slice_fusion.14
  278.7 1.9 constant_dynamic-slice_fusion.14
  283.7 1.9 constant_dynamic-slice_fusion.14
  288.6 1.9 constant_dynamic-slice_fusion.14
  293.6 1.9 constant_dynamic-slice_fusion.14
  298.5 1.9 constant_dynamic-slice_fusion.14
  303.5 1.9 constant_dynamic-slice_fusion.14
  308.4 1.9 constant_dynamic-slice_fusion.14
  313.4 1.9 constant_dynamic-slice_fusion.14
  318.3 1.9 constant_dynamic-slice_fusion.14
  323.3 1.9 constant_dynamic-slice_fusion.14
  328.2 1.9 constant_dynamic-slice_fusion.14
  333.2 1.9 constant_dynamic-slice_fusion.14
  338.1 1.9 constant_dynamic-slice_fusion.14
  372.8 1.9 constant_dynamic-slice_fusion.14
  378.2 42.7 %all-reduce = (f32[]{:T(128)}, f32[]{:T(128)}) all-reduce(f32[]{:T(128)} %get-tuple-element.613, f32[]{:T(128)} %get-tuple-element.612), channel_id=1, replica_groups=mesh['gx'=4,'gy'=4,'gz'=2] {'gx','gy','gz'}, use_global_device_ids=true, to_apply=%region_21.22 | all-reduce | flops 2 | bytes 16 | tf_op jit(solution)/shard_map/psum | solution.py:146
  (1253 shorter events, 241.6 us)
Async XLA Ops:
  1.3 1.0 copy-start
  72.2 2.1 copy-start.1
  72.4 1.8 copy-start.2
  72.4 8.5 %collective-permute-start.6 = (f32[6,1,2,2,128]{4,3,2,0,1:T(2,128)S(1)}, f32[6,1,2,2,128]{4,3,2,0,1:T(2,128)S(1)}, u32[]{:S(2)}, u32[]{:S(2)}) collective-permute-start(f32[6,1,2,2,128]{4,3,2,0,1:T(2,128)S(1)} %bitcast.226), channel_id=1, source_target_pairs={{0,8},{8,16},{16,24},{24,0},{1,9},{9,17},{17,25},{25,1},{2,10},{10... | collective-permute-start | bytes 36872 | tf_op jit(solution)/shard_map/ppermute | solution.py:25
  72.5 8.4 %collective-permute-start.7 = (f32[6,1,2,2,128]{4,3,2,0,1:T(2,128)S(1)}, f32[6,1,2,2,128]{4,3,2,0,1:T(2,128)S(1)}, u32[]{:S(2)}, u32[]{:S(2)}) collective-permute-start(f32[6,1,2,2,128]{4,3,2,0,1:T(2,128)S(1)} %bitcast.227), channel_id=1, source_target_pairs={{8,0},{16,8},{24,16},{0,24},{9,1},{17,9},{25,17},{1,25},{10,2},{18... | collective-permute-start | bytes 36872 | tf_op jit(solution)/shard_map/ppermute | solution.py:27
  74.2 1.8 copy-start.4
  74.2 3.2 collective-permute-start
  74.3 3.1 collective-permute-start.1
  76.0 0.7 copy-start.5
  77.5 7.3 %collective-permute-start.2 = (f32[4,3,1,2,128]{4,3,2,1,0:T(2,128)S(1)}, f32[4,3,1,2,128]{4,3,2,1,0:T(2,128)S(1)}, u32[]{:S(2)}, u32[]{:S(2)}) collective-permute-start(f32[4,3,1,2,128]{4,3,2,1,0:T(2,128)S(1)} %get-tuple-element.693), channel_id=1, source_target_pairs={{0,2},{2,4},{4,6},{6,0},{1,3},{3,5},{5,7},{7,1},{8,10},{10,12},{12... | collective-permute-start | bytes 36872 | tf_op jit(solution)/shard_map/ppermute | solution.py:25
  77.5 7.3 %collective-permute-start.3 = (f32[4,3,1,2,128]{4,3,2,1,0:T(2,128)S(1)}, f32[4,3,1,2,128]{4,3,2,1,0:T(2,128)S(1)}, u32[]{:S(2)}, u32[]{:S(2)}) collective-permute-start(f32[4,3,1,2,128]{4,3,2,1,0:T(2,128)S(1)} %get-tuple-element.694), channel_id=1, source_target_pairs={{2,0},{4,2},{6,4},{0,6},{3,1},{5,3},{7,5},{1,7},{10,8},{12,10},{14... | collective-permute-start | bytes 36872 | tf_op jit(solution)/shard_map/ppermute | solution.py:27
  80.9 6.1 %collective-permute-start.8 = (f32[6,3,1,2,128]{4,3,2,0,1:T(2,128)S(1)}, f32[6,3,1,2,128]{4,3,2,0,1:T(2,128)S(1)}, u32[]{:S(2)}, u32[]{:S(2)}) collective-permute-start(f32[6,3,1,2,128]{4,3,2,0,1:T(2,128)S(1)} %get-tuple-element.691), channel_id=1, source_target_pairs={{0,2},{2,4},{4,6},{6,0},{1,3},{3,5},{5,7},{7,1},{8,10},{10,12},{12... | collective-permute-start | bytes 55304 | tf_op jit(solution)/shard_map/ppermute | solution.py:25
  81.0 6.0 %collective-permute-start.9 = (f32[6,3,1,2,128]{4,3,2,0,1:T(2,128)S(1)}, f32[6,3,1,2,128]{4,3,2,0,1:T(2,128)S(1)}, u32[]{:S(2)}, u32[]{:S(2)}) collective-permute-start(f32[6,3,1,2,128]{4,3,2,0,1:T(2,128)S(1)} %get-tuple-element.692), channel_id=1, source_target_pairs={{2,0},{4,2},{6,4},{0,6},{3,1},{5,3},{7,5},{1,7},{10,8},{12,10},{14... | collective-permute-start | bytes 55304 | tf_op jit(solution)/shard_map/ppermute | solution.py:27
  84.9 4.3 %collective-permute-start.4 = (f32[4,3,4,1,128]{4,3,2,1,0:T(1,128)S(1)}, f32[4,3,4,1,128]{4,3,2,1,0:T(1,128)S(1)}, u32[]{:S(2)}, u32[]{:S(2)}) collective-permute-start(f32[4,3,4,1,128]{4,3,2,1,0:T(1,128)S(1)} %get-tuple-element.687), channel_id=1, source_target_pairs={{0,1},{1,0},{2,3},{3,2},{4,5},{5,4},{6,7},{7,6},{8,9},{9,8},{10,11... | collective-permute-start | bytes 73736 | tf_op jit(solution)/shard_map/ppermute | solution.py:25
  85.0 4.4 %collective-permute-start.5 = (f32[4,3,4,1,128]{4,3,2,1,0:T(1,128)S(1)}, f32[4,3,4,1,128]{4,3,2,1,0:T(1,128)S(1)}, u32[]{:S(2)}, u32[]{:S(2)}) collective-permute-start(f32[4,3,4,1,128]{4,3,2,1,0:T(1,128)S(1)} %get-tuple-element.688), channel_id=1, source_target_pairs={{1,0},{0,1},{3,2},{2,3},{5,4},{4,5},{7,6},{6,7},{9,8},{8,9},{11,10... | collective-permute-start | bytes 73736 | tf_op jit(solution)/shard_map/ppermute | solution.py:27
  87.1 4.0 collective-permute-start.10
  87.2 4.3 %collective-permute-start.11 = (f32[6,3,4,1,128]{4,3,2,0,1:T(1,128)S(1)}, f32[6,3,4,1,128]{4,3,2,0,1:T(1,128)S(1)}, u32[]{:S(2)}, u32[]{:S(2)}) collective-permute-start(f32[6,3,4,1,128]{4,3,2,0,1:T(1,128)S(1)} %get-tuple-element.686), channel_id=1, source_target_pairs={{1,0},{0,1},{3,2},{2,3},{5,4},{4,5},{7,6},{6,7},{9,8},{8,9},{11,10... | collective-permute-start | bytes 110600 | tf_op jit(solution)/shard_map/ppermute | solution.py:27
  91.6 134.4 %copy-start.3 = (f32[6,1,2,2,128]{4,3,2,1,0:T(2,128)S(1)}, f32[6,1,2,2,128]{4,3,2,1,0:T(2,128)}, u32[]{:S(2)}) copy-start(f32[6,1,2,2,128]{4,3,2,1,0:T(2,128)} %param.14) | copy-start | bytes 36868
  226.1 3.2 collective-permute-start.12
  226.1 3.1 collective-permute-start.13
  229.3 5.5 %collective-permute-start.14 = (f32[6,3,1,2,128]{4,3,2,1,0:T(2,128)S(1)}, f32[6,3,1,2,128]{4,3,2,1,0:T(2,128)S(1)}, u32[]{:S(2)}, u32[]{:S(2)}) collective-permute-start(f32[6,3,1,2,128]{4,3,2,1,0:T(2,128)S(1)} %get-tuple-element.689), channel_id=1, source_target_pairs={{0,2},{2,4},{4,6},{6,0},{1,3},{3,5},{5,7},{7,1},{8,10},{10,12},{12... | collective-permute-start | bytes 55304 | tf_op jit(solution)/shard_map/ppermute | solution.py:25
  232.3 5.1 %collective-permute-start.15 = (f32[6,3,1,2,128]{4,3,2,1,0:T(2,128)S(1)}, f32[6,3,1,2,128]{4,3,2,1,0:T(2,128)S(1)}, u32[]{:S(2)}, u32[]{:S(2)}) collective-permute-start(f32[6,3,1,2,128]{4,3,2,1,0:T(2,128)S(1)} %get-tuple-element.690), channel_id=1, source_target_pairs={{2,0},{4,2},{6,4},{0,6},{3,1},{5,3},{7,5},{1,7},{10,8},{12,10},{14... | collective-permute-start | bytes 55304 | tf_op jit(solution)/shard_map/ppermute | solution.py:27
  237.5 4.0 collective-permute-start.16
  239.2 4.0 collective-permute-start.17
